TPU v7x, 256 devices: a whole 4x4x8 slice. The times are simulated.
256 devices in a mesh: patch: 32 (over x, z_hi, core), tp: 8 (over y, z_lo).
Axes of the slice: x: 4, y: 4, z: 8 (z_hi: 4, z_lo: 2; z = z_hi * 2 + z_lo), core: 2. Of those that a mesh axis runs over, the one named last changes fastest.
Arguments:
- resid_corrupt: bfloat16 [512, 4096], P(None, 'tp'), may hold values from -6 to 6
- resid_clean: bfloat16 [2, 512, 4096], P(None, 'patch', 'tp'), may hold values from -6 to 6
- patch_level: int32 [32], P('patch'), may hold values from 0 to 1
- patch_mask: int32 [32, 128], P('patch'), may hold values 0 or 1
- norm_gain: bfloat16 [4096], P('tp'), may hold values from 0.099609375 to 1.8984375
- final_gain: bfloat16 [4096], P('tp'), may hold values from 0.099609375 to 1.8984375
- w_query: bfloat16 [4096, 4096], P('patch', 'tp'), may hold values from -1 to 1
- w_key: bfloat16 [4096, 1024], P('patch', 'tp'), may hold values from -1 to 1
- w_value: bfloat16 [4096, 1024], P('patch', 'tp'), may hold values from -0.09375 to 0.09375
- w_out: bfloat16 [4096, 4096], P('tp', 'patch'), may hold values from -0.09375 to 0.09375
- unembed: bfloat16 [128256, 4096], P(('patch', 'tp')), may hold values from -0.09375 to 0.09375
- scored_ids: int32 [256], replicated, may hold values from 0 to 128255
- base_logits: float32 [512, 256], P('tp'), may hold values from -6 to 6
Outputs:
- logit_shift: float32 [32, 512, 256], P('patch', 'tp')
All inputs are finite; a program needn't handle non-finite values. No bound on the sum of `patch_mask` on one device may be relied on, other than what follows from the above.
Results may differ from a plain program's by a relative error of at most 0.01.
The roundings to bfloat16 on the way count: a program that leaves them out, or rounds other values in their place, can miss the bound.
Values may be sent and summed in bfloat16 or wider, within the bound.
A program may use at most 128 MiB of HBM per device.

v0:
```python
import jax
import jax.numpy as jnp
from jax import lax
from jax.sharding import PartitionSpec as P

D = 4096
HD = 128
SEQ = 128
PROMPTS = 4
EPSILON = 1e-05
THETA = 500000.0


def in_one_piece(arrays, axis, dim, along):
    both = jnp.concatenate(arrays, axis=along)
    out, at, gathered = (lax.all_gather(both, axis, axis=dim, tiled=True), 0, [])
    for a in arrays:
        gathered.append(lax.slice_in_dim(out, at, at + a.shape[along], axis=along))
        at += a.shape[along]
    return tuple(gathered)


def in_blocks(value, dim, peers):
    dims = value.shape
    pieces = value.reshape(*dims[:dim], peers, dims[dim] // peers, *dims[dim + 1 :])
    return jnp.moveaxis(pieces, dim, 0)


def summed_on_arrival(value, axis, dim):
    pieces = in_blocks(value, dim, lax.axis_size(axis))
    arrived = lax.all_to_all(pieces, axis, split_axis=0, concat_axis=0, tiled=True)
    return arrived.astype(jnp.float32).sum(axis=0)


def total_of_pieces(value, axis):
    pieces = lax.all_gather(value, axis).astype(jnp.float32)
    return pieces.sum(axis=0)


def rope_tables(length, head_dim):
    half = head_dim // 2
    freqs = THETA ** (-(jnp.arange(half, dtype=jnp.float32) * 2.0 / head_dim))
    angles = jnp.arange(length, dtype=jnp.float32)[:, None] * freqs[None, :]
    return (jnp.cos(angles)[:, None, :], jnp.sin(angles)[:, None, :])


def rotate(values, cosine, sine):
    half = values.shape[-1] // 2
    lower = values[..., :half]
    upper = values[..., half:]
    return jnp.concatenate([lower * cosine - upper * sine, upper * cosine + lower * sine], axis=-1)


def rms_scale(rows, gain):
    return rows * lax.rsqrt(jnp.mean(rows * rows, axis=-1, keepdims=True) + EPSILON) * gain


def attend(query_f, key_f, value_f):
    heads = query_f.shape[1] // HD
    kv_heads = key_f.shape[1] // HD
    group = heads // kv_heads
    prompts = query_f.shape[0] // SEQ
    cosine, sine = rope_tables(SEQ, HD)
    queries = rotate(query_f.reshape(prompts, SEQ, heads, HD), cosine, sine).astype(jnp.bfloat16)
    queries = queries.reshape(prompts, SEQ, kv_heads, group, HD)
    key_rows = rotate(key_f.reshape(prompts, SEQ, kv_heads, HD), cosine, sine).astype(jnp.bfloat16)
    value_rows = value_f.astype(jnp.bfloat16).reshape(prompts, SEQ, kv_heads, HD)
    scores = jnp.einsum(
        "pqkgd,pskd->pkgqs", queries, key_rows, preferred_element_type=jnp.float32
    ) * HD ** (-0.5)
    causal = lax.iota(jnp.int32, SEQ)[:, None] >= lax.iota(jnp.int32, SEQ)[None, :]
    scores = jnp.where(causal, scores, -1e30)
    probs = jax.nn.softmax(scores, axis=-1).astype(jnp.bfloat16)
    attended = jnp.einsum(
        "pkgqs,pskd->pqkgd", probs, value_rows, preferred_element_type=jnp.float32
    )
    return attended.astype(jnp.bfloat16).reshape(prompts * SEQ, heads * HD)


def on_device(
    resid_corrupt,
    resid_clean,
    patch_level,
    patch_mask,
    norm_gain,
    final_gain,
    w_query,
    w_key,
    w_value,
    w_out,
    unembed,
    scored_ids,
    base_logits,
):
    level = patch_level[0]
    row_mask = jnp.tile(patch_mask[0], PROMPTS) == 1
    clean_all = lax.all_gather(resid_clean, "patch", axis=1, tiled=True)
    early = (row_mask & (level == 0))[:, None]
    layer_in = jnp.where(early, clean_all[0], resid_corrupt)
    full_rows, full_gain = (
        lax.all_gather(layer_in, "tp", axis=1, tiled=True),
        lax.all_gather(norm_gain, "tp", axis=0, tiled=True),
    )
    normed = rms_scale(full_rows.astype(jnp.float32), full_gain.astype(jnp.float32)).astype(
        jnp.bfloat16
    )
    pieces = in_one_piece((w_query, w_key, w_value), "patch", 0, 1)
    query_f = jnp.dot(normed, pieces[0], preferred_element_type=jnp.float32)
    key_f = jnp.dot(normed, pieces[1], preferred_element_type=jnp.float32)
    value_f = jnp.dot(normed, pieces[2], preferred_element_type=jnp.float32)
    attended = attend(query_f, key_f, value_f)
    partial_out = jnp.dot(
        attended,
        lax.all_gather(w_out, "patch", axis=1, tiled=True),
        preferred_element_type=jnp.float32,
    )
    head_block = summed_on_arrival(partial_out.astype(jnp.bfloat16), "tp", 1)
    middle = layer_in.astype(jnp.float32) + head_block
    late = (row_mask & (level == 1))[:, None]
    residual = jnp.where(late, clean_all[1].astype(jnp.float32), middle)
    squares = lax.psum(jnp.sum(residual * residual, axis=1), "tp")
    scaling = lax.rsqrt(squares / D + EPSILON)[:, None]
    final_block = (residual * scaling * final_gain.astype(jnp.float32)).astype(jnp.bfloat16)
    rows_dev = unembed.shape[0]
    first_row = lax.axis_index(("patch", "tp")) * rows_dev
    owned_rows = (scored_ids[:, None] == first_row + lax.iota(jnp.int32, rows_dev)[None, :]).astype(
        jnp.bfloat16
    )
    picked = jnp.dot(owned_rows, unembed, preferred_element_type=jnp.float32)
    spread = summed_on_arrival(picked.astype(jnp.bfloat16), "tp", 1)
    score_block = (
        total_of_pieces(spread.astype(jnp.bfloat16), "patch")
        .astype(jnp.float32)
        .astype(jnp.bfloat16)
    )
    partial_logits = jnp.einsum(
        "td,sd->ts", final_block, score_block, preferred_element_type=jnp.float32
    )
    token_logits = summed_on_arrival(partial_logits.astype(jnp.bfloat16), "tp", 0)
    return (token_logits - base_logits)[None]


def solution(mesh):
    placed = (
        P(None, "tp"),
        P(None, "patch", "tp"),
        P("patch"),
        P("patch", None),
        P("tp"),
        P("tp"),
        P("patch", "tp"),
        P("patch", "tp"),
        P("patch", "tp"),
        P("tp", "patch"),
        P(("patch", "tp"), None),
        P(),
        P("tp", None),
    )
    return jax.shard_map(
        on_device, mesh=mesh, in_specs=placed, out_specs=P("patch", "tp", None), check_vma=False
    )
```

profile of v0, /device:TPU:2, one launch (start us, length us, event | category | flops | bytes accessed | tf_op | source)
XLA Modules:
  0.0 461.8 jit_solution(4920440208380993172)
XLA Ops:
  6.5 0.7 all-gather.8.cloned.1.call-update
  8.6 55.1 %all-gather.8.cloned.1.call-done = bf16[2,512,512]{2,1,0:T(8,128)(2,1)} async-done(((bf16[2,16,512]{2,1,0:T(8,128)(2,1)}), bf16[2,512,512]{2,1,0:T(8,128)(2,1)}) %all-gather.8.cloned.1.call-update) | async-done | bytes 1048592 | tf_op jit(solution)/shard_map/all_gather | solution.py:97
  63.7 2.1 fusion.14
  65.9 1.7 pad_maximum_fusion
  68.2 3.5 convolution_convert_fusion.1
  72.0 54.5 %all_to_all.15 = bf16[8,256,512]{2,1,0:T(8,128)(2,1)S(1)} all-to-all(bf16[8,256,512]{2,1,0:T(8,128)(2,1)S(1)} %bitcast.85), channel_id=1, replica_groups=mesh['patch'=32,'tp'=8] {'tp'}, dimensions={0} | all-to-all | bytes 4194304 | tf_op jit(solution)/shard_map/all_to_all | solution.py:31
  126.5 1.1 reduce_sum.73
  127.6 25.7 %all-gather.1 = bf16[8,1,512]{2,1,0:T(2,128)(2,1)S(1)} all-gather(bf16[1,1,512]{2,1,0:T(2,128)(2,1)S(1)} %reshape.154), channel_id=1, replica_groups=mesh['patch'=32,'tp'=8] {'tp'}, dimensions={0}, use_global_device_ids=true | all-gather | bytes 9216 | tf_op jit(solution)/shard_map/all_gather | solution.py:102
  153.6 27.4 %all-gather.10.cloned.1.call-done = bf16[512,4096]{1,0:T(8,128)(2,1)} async-done(((bf16[512,512]{1,0:T(8,128)(2,1)}), bf16[512,4096]{1,0:T(8,128)(2,1)}) %all-gather.10.cloned.1.call-update) | async-done | bytes 4194320 | tf_op jit(solution)/shard_map/all_gather | solution.py:101
  181.0 3.1 fusion
  184.1 67.0 %all-gather.12.cloned.1.call-done = bf16[4096,768]{1,0:T(8,128)(2,1)} async-done(((bf16[128,768]{1,0:T(8,128)(2,1)}), bf16[4096,768]{1,0:T(8,128)(2,1)}) %all-gather.12.cloned.1.call-update) | async-done | bytes 6291472 | tf_op jit(solution)/shard_map/all_gather | solution.py:16
  251.1 5.8 %fusion.3 = f32[512,512]{1,0:T(8,128)S(1)} fusion(bf16[4096,768]{1,0:T(8,128)(2,1)} %all-gather.12.cloned.1.call-done, bf16[512,4096]{1,0:T(8,128)(2,1)} %all-gather.10.cloned.1.call-done, f32[4096]{0:T(1024)S(1)} %bitcast.91, f32[512]{0:T(512)S(1)} %add_rsqrt_fusion.1), kind=kOutput, calls=%fused_computation.9 | convolution fusion | flops 2155872256 | bytes 9455616 | tf_op jit(solution)/shard_map/dot_general | solution.py:108
  257.3 3.8 fusion.8
  262.9 1.2 copy-done.1
  264.1 2.6 convolution_convert_fusion.4
  267.4 48.2 %all-gather.14.cloned.1.call-done = bf16[512,4096]{1,0:T(8,128)(2,1)} async-done(((bf16[512,128]{1,0:T(8,128)(2,1)}), bf16[512,4096]{1,0:T(8,128)(2,1)}) %all-gather.14.cloned.1.call-update) | async-done | bytes 4194320 | tf_op jit(solution)/shard_map/all_gather | solution.py:114
  315.5 4.5 convolution_convert_fusion
  320.1 2.3 copy.57
  322.4 5.0 %all-to-all-start = ((bf16[8,512,512]{2,1,0:T(8,128)(2,1)}), bf16[8,512,512]{2,1,0:T(8,128)(2,1)}, u32[]{:S(2)}, u32[]{:S(2)}) async-start(bf16[8,512,512]{2,1,0:T(8,128)(2,1)} %bitcast.83), calls=%async_computation | async-start | bytes 8388608 | tf_op jit(solution)/shard_map/all_to_all | solution.py:31
  327.4 92.0 %all-to-all-done = bf16[8,512,512]{2,1,0:T(8,128)(2,1)} async-done(((bf16[8,512,512]{2,1,0:T(8,128)(2,1)}), bf16[8,512,512]{2,1,0:T(8,128)(2,1)}, u32[]{:S(2)}, u32[]{:S(2)}) %all-to-all-start) | async-done | bytes 4194336 | tf_op jit(solution)/shard_map/all_to_all | solution.py:31
  419.5 2.9 convert_reduce_fusion
  422.7 16.9 %psum.7 = f32[512]{0:T(512)S(1)} all-reduce(f32[512]{0:T(512)S(1)} %multiply_reduce_fusion), channel_id=1, replica_groups=mesh['patch'=32,'tp'=8] {'tp'}, use_global_device_ids=true, to_apply=%region_5.6 | all-reduce | flops 512 | bytes 4096 | tf_op jit(solution)/shard_map/psum | solution.py:121
  439.6 4.8 %reduce_sum.74 = bf16[256,512]{1,0:T(8,128)(2,1)S(1)} reduce(bf16[32,256,512]{2,1,0:T(8,128)(2,1)} %bitcast.84, bf16[]{:T(256)} %constant.47.clone.1), dimensions={0}, to_apply=%region_7.8 | reduce | flops 4063232 | bytes 8650754 | tf_op jit(solution)/shard_map/reduce_sum | solution.py:37
  444.9 9.7 %all_to_all.16 = bf16[8,64,256]{2,1,0:T(8,128)(2,1)S(1)} all-to-all(bf16[8,64,256]{2,1,0:T(8,128)(2,1)S(1)} %bitcast.90), channel_id=1, replica_groups=mesh['patch'=32,'tp'=8] {'tp'}, dimensions={0} | all-to-all | bytes 524288 | tf_op jit(solution)/shard_map/all_to_all | solution.py:31
  (46 shorter events, 6.2 us)
Async XLA Ops:
  6.5 57.2 %all-gather.8.cloned.1.call-start = ((), (), s32[]{:S(2)}) async-start(), calls=%async_computation.3 | async-start | bytes 1081344 | tf_op jit(solution)/shard_map/all_gather | solution.py:97
  7.3 173.8 %all-gather.10.cloned.1.call-start = ((), (), s32[]{:S(2)}) async-start(), calls=%async_computation.4 | async-start | bytes 4718592 | tf_op jit(solution)/shard_map/all_gather | solution.py:101
  65.9 185.3 %all-gather.12.cloned.1.call-start = ((), (), s32[]{:S(2)}) async-start(), calls=%async_computation.5 | async-start | bytes 6488064 | tf_op jit(solution)/shard_map/all_gather | solution.py:16
  67.6 247.9 %all-gather.14.cloned.1.call-start = ((), (), s32[]{:S(2)}) async-start(), calls=%async_computation.6 | async-start | bytes 4325376 | tf_op jit(solution)/shard_map/all_gather | solution.py:114
  68.2 371.4 %all-gather.16.cloned.1.call-start = ((), (), s32[]{:S(2)}) async-start(), calls=%async_computation.7 | async-start | bytes 8650752 | tf_op jit(solution)/shard_map/all_gather | solution.py:36
  72.0 55.6 %copy-start.4 = (bf16[512]{0:T(512)(128)(2,1)S(1)}, bf16[512]{0:T(512)(128)(2,1)}, u32[]{:S(2)}) copy-start(bf16[512]{0:T(512)(128)(2,1)} %param.17) | copy-start | bytes 3076
  261.9 2.2 copy-start.1
  322.4 5.0 %copy-start.5 = (bf16[512]{0:T(512)(128)(2,1)S(1)}, bf16[512]{0:T(512)(128)(2,1)}, u32[]{:S(2)}) copy-start(bf16[512]{0:T(512)(128)(2,1)} %param.18) | copy-start | bytes 3076
  322.4 97.0 %all-to-all-start = ((bf16[8,512,512]{2,1,0:T(8,128)(2,1)}), bf16[8,512,512]{2,1,0:T(8,128)(2,1)}, u32[]{:S(2)}, u32[]{:S(2)}) async-start(bf16[8,512,512]{2,1,0:T(8,128)(2,1)} %bitcast.83), calls=%async_computation | async-start | bytes 8388608 | tf_op jit(solution)/shard_map/all_to_all | solution.py:31
  327.4 94.9 %copy-start = (bf16[512,512]{1,0:T(8,128)(2,1)S(1)}, bf16[512,512]{1,0:T(8,128)(2,1)}, u32[]{:S(2)}) copy-start(bf16[512,512]{1,0:T(8,128)(2,1)} %fusion.14) | copy-start | bytes 1572868
  327.4 94.9 %copy-start.2 = (bf16[2,512,512]{2,1,0:T(8,128)(2,1)S(1)}, bf16[2,512,512]{2,1,0:T(8,128)(2,1)}, u32[]{:S(2)}) copy-start(bf16[2,512,512]{2,1,0:T(8,128)(2,1)} %all-gather.8.cloned.1.call-done) | copy-start | bytes 3145732
  439.6 15.0 %copy-start.3 = (f32[64,256]{1,0:T(8,128)S(1)}, f32[64,256]{1,0:T(8,128)}, u32[]{:S(2)}) copy-start(f32[64,256]{1,0:T(8,128)} %param.25) | copy-start | bytes 196612
Sparse Core Ops, SparseCore 0:
  10.0 53.6 all-gather.7
  66.0 115.0 all-gather.9
  183.6 67.4 all-gather.11
  253.4 62.0 all-gather.13
  317.9 95.5 all-gather.15
where the time goes:
time: 462 us
  waiting for transfers between devices  291 us (63%)
  blocking collectives  107 us (23%)
  matrix products  21.6 us (5%)
  other arithmetic  18.2 us (4%)
  between operations  14 us (3%)
  starting transfers between devices  5.12 us (1%)
  local copies, waits for them, and re-layouts  5.11 us (1%)
    all_to_all x1, waiting for transfers between devices, summed_on_arrival(): lax.all_to_all(pieces, axis, split_axis=0, concat_axis=0, tiled=True)  92 us
    all_gather x1, waiting for transfers between devices, in_one_piece(): lax.all_gather(both, axis, axis=dim, tiled=True)  67 us
    all_to_all x2, blocking collectives, summed_on_arrival(): lax.all_to_all(pieces, axis, split_axis=0, concat_axis=0, tiled=True)  64.2 us
    all_gather x1, waiting for transfers between devices, on_device(): clean_all = lax.all_gather(resid_clean, 'patch', axis=1, tiled=True)  55.1 us
    all_gather x1, waiting for transfers between devices, on_device(): lax.all_gather(w_out, 'patch', axis=1, tiled=True)  48.2 us
    all_gather x1, waiting for transfers between devices, on_device(): lax.all_gather(layer_in, 'tp', axis=1, tiled=True)  27.4 us
    all_gather x1, blocking collectives, on_device(): lax.all_gather(norm_gain, 'tp', axis=0, tiled=True)  25.7 us
    psum x1, blocking collectives, on_device(): squares = lax.psum(jnp.sum(residual * residual, axis=1), 'tp')  16.9 us
  transfers between devices with their start and end apart: 6, of which 5 were waited for; matrix products, arithmetic and copies ran while one was open for 8% of the time, Pallas kernels for 0%

commit v1 on v0

--- a/solution.py
+++ b/solution.py
@@ -98,7 +98,9 @@
     early = (row_mask & (level == 0))[:, None]
     layer_in = jnp.where(early, clean_all[0], resid_corrupt)
     full_rows, full_gain = (
-        lax.all_gather(layer_in, "tp", axis=1, tiled=True),
+        jnp.concatenate(
+            lax.all_to_all(jnp.stack([layer_in] * lax.axis_size("tp")), "tp", 0, 0), axis=1
+        ),
         lax.all_gather(norm_gain, "tp", axis=0, tiled=True),
     )
     normed = rms_scale(full_rows.astype(jnp.float32), full_gain.astype(jnp.float32)).astype(

time: 462 us -> 372 us (0.81)
  waiting for transfers between devices: 291 us -> 122 us
  local copies, waits for them, and re-layouts: 5.11 us -> 48.1 us
  blocking collectives: 107 us -> 124 us
  other arithmetic: 18.2 us -> 28.8 us
  starting transfers between devices: 5.12 us -> 15.6 us
    all_gather x1, blocking collectives: 25.7 us -> 97.5 us  [on_device(): lax.all_gather(norm_gain, 'tp', axis=0, tiled=True)]
    all_gather x1, waiting for transfers between devices: 67 us -> 0.01 us  [in_one_piece(): lax.all_gather(both, axis, axis=dim, tiled=True)]
    all_to_all x2 -> x1, blocking collectives: 64.2 us -> 10.1 us  [summed_on_arrival(): lax.all_to_all(pieces, axis, split_axis=0, concat_axis=0, tiled=True)]
    all_gather x1, waiting for transfers between devices: 48.2 us -> 0.02 us  [on_device(): lax.all_gather(w_out, 'patch', axis=1, tiled=True)]
    all_gather x1 -> x0, waiting for transfers between devices: 27.4 us -> none  [on_device(): lax.all_gather(layer_in, 'tp', axis=1, tiled=True)]
    convert_element_type x0 -> x3, local copies, waits for them, and re-layouts: none -> 27 us  [the longest x2 20 us: on_device(): full_rows.astype(jnp.float32)]
    all_gather x1, waiting for transfers between devices: 55.1 us -> 40.6 us  [on_device(): clean_all = lax.all_gather(resid_clean, 'patch', axis=1, tiled=True)]
    all_to_all x1 -> x2, waiting for transfers between devices: 92 us -> 80.1 us  [summed_on_arrival(): lax.all_to_all(pieces, axis, split_axis=0, concat_axis=0, tiled=True)]
  transfers between devices with their start and end apart: 6 -> 7, of which waited for: 5 -> 2; matrix products, arithmetic and copies ran while one was open for 8% -> 23% of each run, Pallas kernels for 0% -> 0%
where the time goes in v1:
time: 372 us; the launch traced here: 371 us
  blocking collectives  124 us (33%)
  waiting for transfers between devices  122 us (33%)
  local copies, waits for them, and re-layouts  48.1 us (13%)
  other arithmetic  28.8 us (8%)
  matrix products  18 us (5%)
  starting transfers between devices  15.6 us (4%)
  between operations  14.1 us (4%)
    all_gather x1, blocking collectives, on_device(): lax.all_gather(norm_gain, 'tp', axis=0, tiled=True)  97.5 us
    all_to_all x2, waiting for transfers between devices, summed_on_arrival(): lax.all_to_all(pieces, axis, split_axis=0, concat_axis=0, tiled=True)  80.1 us
    all_gather x1, waiting for transfers between devices, on_device(): clean_all = lax.all_gather(resid_clean, 'patch', axis=1, tiled=True)  40.6 us
    convert_element_type x2, local copies, waits for them, and re-layouts, on_device(): full_rows.astype(jnp.float32)  20 us
    psum x1, blocking collectives, on_device(): squares = lax.psum(jnp.sum(residual * residual, axis=1), 'tp')  16.3 us
    all_to_all x2, starting transfers between devices, summed_on_arrival(): lax.all_to_all(pieces, axis, split_axis=0, concat_axis=0, tiled=True)  10.8 us
    all_to_all x1, blocking collectives, summed_on_arrival(): lax.all_to_all(pieces, axis, split_axis=0, concat_axis=0, tiled=True)  10.1 us
    unnamed x25, local copies, waits for them, and re-layouts  7.94 us
  transfers between devices with their start and end apart: 7, of which 2 were waited for; matrix products, arithmetic and copies ran while one was open for 23% of the time, Pallas kernels for 0%

profile of v1, /device:TPU:2, one launch (start us, length us, event | category | flops | bytes accessed | tf_op | source)
XLA Modules:
  0.0 370.8 jit_solution(13818816652168625694)
XLA Ops:
  10.8 3.5 convolution_convert_fusion.1
  15.9 5.8 %all-to-all-start.2 = ((bf16[8,256,512]{2,1,0:T(8,128)(2,1)}), bf16[8,256,512]{2,1,0:T(8,128)(2,1)S(1)}, u32[]{:S(2)}, u32[]{:S(2)}) async-start(bf16[8,256,512]{2,1,0:T(8,128)(2,1)} %bitcast.117), calls=%async_computation.2 | async-start | bytes 4194304 | tf_op jit(solution)/shard_map/all_to_all | solution.py:31
  23.2 40.6 %all-gather.7.cloned.1.call-done = bf16[2,512,512]{2,1,0:T(8,128)(2,1)} async-done(((bf16[2,16,512]{2,1,0:T(8,128)(2,1)}), bf16[2,512,512]{2,1,0:T(8,128)(2,1)}) %all-gather.7.cloned.1.call-update) | async-done | bytes 1048592 | tf_op jit(solution)/shard_map/all_gather | solution.py:97
  67.3 4.7 %all-to-all-start = ((bf16[8,512,512]{2,1,0:T(8,128)(2,1)}), bf16[8,512,512]{2,1,0:T(8,128)(2,1)}, u32[]{:S(2)}, u32[]{:S(2)}) async-start(bf16[8,512,512]{2,1,0:T(8,128)(2,1)} %stack.2), calls=%async_computation | async-start | bytes 8388608 | tf_op jit(solution)/shard_map/all_to_all | solution.py:102
  73.2 97.5 %all-gather.1 = bf16[8,1,512]{2,1,0:T(2,128)(2,1)S(1)} all-gather(bf16[1,1,512]{2,1,0:T(2,128)(2,1)S(1)} %reshape.207), channel_id=1, replica_groups=mesh['patch'=32,'tp'=8] {'tp'}, dimensions={0}, use_global_device_ids=true | all-gather | bytes 9216 | tf_op jit(solution)/shard_map/all_gather | solution.py:104
  170.9 6.6 %copy.52 = bf16[8,512,512]{1,2,0:T(8,128)(2,1)} copy(bf16[8,512,512]{2,1,0:T(8,128)(2,1)} %all-to-all-done) | data formatting | bytes 8388608 | tf_op jit(solution)/shard_map/all_to_all | solution.py:102
  177.6 6.6 %convert_bitcast_fusion = f32[512,8,512]{0,2,1:T(8,128)} fusion(bf16[8,512,512]{1,2,0:T(8,128)(2,1)} %copy.52), kind=kLoop, calls=%fused_computation.7 | loop fusion | flops 2097152 | bytes 12582912 | tf_op jit(solution)/shard_map/convert_element_type | solution.py:106
  184.1 9.9 %reshape.216 = f32[4,128,4096]{1,0,2:T(4,128)} reshape(f32[512,8,512]{0,2,1:T(8,128)} %convert_bitcast_fusion) | data formatting | bytes 16777216 | tf_op jit(solution)/shard_map/convert_element_type | solution.py:106
  194.1 10.1 %copy.72 = f32[4,128,4096]{2,1,0:T(8,128)} copy(f32[4,128,4096]{1,0,2:T(4,128)} %reshape.216) | data formatting | bytes 16777216 | tf_op jit(solution)/shard_map/convert_element_type | solution.py:106
  204.2 3.3 multiply_reduce_fusion
  207.6 2.6 fusion.3
  210.2 7.0 %reshape.217 = bf16[4,128,4096]{1,0,2:T(4,128)(2,1)} reshape(bf16[512,8,512]{0,2,1:T(8,128)(2,1)} %fusion.3) | data formatting | bytes 8388608 | tf_op jit(solution)/shard_map/convert_element_type | solution.py:106
  217.1 4.2 %fusion.1 = bf16[512,4096]{0,1:T(8,128)(2,1)} fusion(bf16[8,512,512]{1,2,0:T(8,128)(2,1)} %copy.52, f32[4096]{0:T(1024)S(1)} %bitcast.124, f32[512]{0:T(512)S(1)} %get-tuple-element.10), kind=kLoop, calls=%fused_computation.2 | loop fusion | flops 8388608 | bytes 8407040 | tf_op jit(solution)/shard_map/convert_element_type | solution.py:106
  221.3 2.8 copy-done.1
  224.1 5.2 %fusion.11 = f32[4,128,1,128]{1,3,0,2:T(8,128)S(1)} fusion(f32[4,128,4096]{2,1,0:T(8,128)} %copy.72, f32[4096]{0:T(1024)S(1)} %bitcast.125, f32[4,128]{1,0:T(4,128)S(1)} %get-tuple-element.9, bf16[4096,768]{0,1:T(8,128)(2,1)S(1)} %copy-done.1), kind=kOutput, calls=%fused_computation.24 | convolution fusion | flops 543162368 | bytes 9717760 | tf_op jit(solution)/shard_map/dot_general | solution.py:111
  229.9 2.3 fusion.4
  236.6 4.5 %convolution_convert_fusion = bf16[512,4096]{1,0:T(8,128)(2,1)S(1)} fusion(bf16[512,4096]{1,0:T(8,128)(2,1)} %all-gather.11.cloned.1.call-done, bf16[64,8,4,128]{3,2,1,0:T(4,128)(2,1)S(1)} %bitcast.122), kind=kOutput, calls=%fused_computation.8 | convolution fusion | flops 2149580800 | bytes 8912896 | tf_op jit(solution)/shard_map/dot_general | solution.py:114
  241.1 2.3 copy.91
  243.5 5.0 %all-to-all-start.1 = ((bf16[8,512,512]{2,1,0:T(8,128)(2,1)}), bf16[8,512,512]{2,1,0:T(8,128)(2,1)}, u32[]{:S(2)}, u32[]{:S(2)}) async-start(bf16[8,512,512]{2,1,0:T(8,128)(2,1)} %bitcast.115), calls=%async_computation.1 | async-start | bytes 8388608 | tf_op jit(solution)/shard_map/all_to_all | solution.py:31
  248.5 80.1 %all-to-all-done.1 = bf16[8,512,512]{2,1,0:T(8,128)(2,1)} async-done(((bf16[8,512,512]{2,1,0:T(8,128)(2,1)}), bf16[8,512,512]{2,1,0:T(8,128)(2,1)}, u32[]{:S(2)}, u32[]{:S(2)}) %all-to-all-start.1) | async-done | bytes 4194336 | tf_op jit(solution)/shard_map/all_to_all | solution.py:31
  328.6 2.9 convert_reduce_fusion
  331.9 16.3 %psum.7 = f32[512]{0:T(512)S(1)} all-reduce(f32[512]{0:T(512)S(1)} %multiply_reduce_fusion.1), channel_id=1, replica_groups=mesh['patch'=32,'tp'=8] {'tp'}, use_global_device_ids=true, to_apply=%region_5.6 | all-reduce | flops 512 | bytes 4096 | tf_op jit(solution)/shard_map/psum | solution.py:123
  348.2 4.8 %reduce_sum.74 = bf16[256,512]{1,0:T(8,128)(2,1)S(1)} reduce(bf16[32,256,512]{2,1,0:T(8,128)(2,1)} %bitcast.116, bf16[]{:T(256)} %constant.47.clone.1), dimensions={0}, to_apply=%region_7.8 | reduce | flops 4063232 | bytes 8650754 | tf_op jit(solution)/shard_map/reduce_sum | solution.py:37
  353.5 10.1 %all_to_all.20 = bf16[8,64,256]{2,1,0:T(8,128)(2,1)S(1)} all-to-all(bf16[8,64,256]{2,1,0:T(8,128)(2,1)S(1)} %bitcast.123), channel_id=1, replica_groups=mesh['patch'=32,'tp'=8] {'tp'}, dimensions={0} | all-to-all | bytes 524288 | tf_op jit(solution)/shard_map/all_to_all | solution.py:31
  (66 shorter events, 17.9 us)
Async XLA Ops:
  6.5 57.3 %all-gather.7.cloned.1.call-start = ((), (), s32[]{:S(2)}) async-start(), calls=%async_computation.4 | async-start | bytes 1081344 | tf_op jit(solution)/shard_map/all_gather | solution.py:97
  7.3 214.0 %all-gather.9.cloned.1.call-start = ((), (), s32[]{:S(2)}) async-start(), calls=%async_computation.5 | async-start | bytes 6488064 | tf_op jit(solution)/shard_map/all_gather | solution.py:16
  14.4 8.8 %copy-start.9 = (s32[1,128]{1,0:T(1,128)S(1)}, s32[1,128]{1,0:T(1,128)}, u32[]{:S(2)}) copy-start(s32[1,128]{1,0:T(1,128)} %param.16) | copy-start | bytes 1540
  14.4 49.4 %copy-start.5 = (bf16[512,512]{1,0:T(8,128)(2,1)S(1)}, bf16[512,512]{1,0:T(8,128)(2,1)}, u32[]{:S(2)}) copy-start(bf16[512,512]{1,0:T(8,128)(2,1)} %param.13) | copy-start | bytes 1572868
  15.9 49.1 %all-to-all-start.2 = ((bf16[8,256,512]{2,1,0:T(8,128)(2,1)}), bf16[8,256,512]{2,1,0:T(8,128)(2,1)S(1)}, u32[]{:S(2)}, u32[]{:S(2)}) async-start(bf16[8,256,512]{2,1,0:T(8,128)(2,1)} %bitcast.117), calls=%async_computation.2 | async-start | bytes 4194304 | tf_op jit(solution)/shard_map/all_to_all | solution.py:31
  21.7 214.8 %all-gather.11.cloned.1.call-start = ((), (), s32[]{:S(2)}) async-start(), calls=%async_computation.6 | async-start | bytes 4325376 | tf_op jit(solution)/shard_map/all_gather | solution.py:116
  67.3 5.9 %copy-start.7 = (bf16[512]{0:T(512)(128)(2,1)S(1)}, bf16[512]{0:T(512)(128)(2,1)}, u32[]{:S(2)}) copy-start(bf16[512]{0:T(512)(128)(2,1)} %param.17) | copy-start | bytes 3076
  67.3 103.6 %all-to-all-start = ((bf16[8,512,512]{2,1,0:T(8,128)(2,1)}), bf16[8,512,512]{2,1,0:T(8,128)(2,1)}, u32[]{:S(2)}, u32[]{:S(2)}) async-start(bf16[8,512,512]{2,1,0:T(8,128)(2,1)} %stack.2), calls=%async_computation | async-start | bytes 8388608 | tf_op jit(solution)/shard_map/all_to_all | solution.py:102
  72.0 276.2 %all-gather.13.cloned.1.call-start = ((), (), s32[]{:S(2)}) async-start(), calls=%async_computation.7 | async-start | bytes 8650752 | tf_op jit(solution)/shard_map/all_gather | solution.py:36
  204.2 3.4 copy-start
  221.3 2.8 copy-start.1
  224.1 5.2 %slice-start = ((bf16[4096,768]{0,1:T(8,128)(2,1)}), bf16[4096,512]{0,1:T(8,128)(2,1)S(1)}, s32[]{:S(2)}) async-start(bf16[4096,768]{0,1:T(8,128)(2,1)} %all-gather.9.cloned.1.call-done), calls=%async_computation.8 | async-start | bytes 8388608 | tf_op jit(solution)/shard_map/slice | solution.py:18
  224.1 5.9 %copy-start.3 = (bf16[4,128,4096]{1,0,2:T(4,128)(2,1)S(1)}, bf16[4,128,4096]{1,0,2:T(4,128)(2,1)}, u32[]{:S(2)}) copy-start(bf16[4,128,4096]{1,0,2:T(4,128)(2,1)} %reshape.217) | copy-start | bytes 12582916
  232.3 2.3 copy-start.2
  243.5 5.0 %copy-start.8 = (bf16[512]{0:T(512)(128)(2,1)S(1)}, bf16[512]{0:T(512)(128)(2,1)}, u32[]{:S(2)}) copy-start(bf16[512]{0:T(512)(128)(2,1)} %param.18) | copy-start | bytes 3076
  243.5 85.1 %all-to-all-start.1 = ((bf16[8,512,512]{2,1,0:T(8,128)(2,1)}), bf16[8,512,512]{2,1,0:T(8,128)(2,1)}, u32[]{:S(2)}, u32[]{:S(2)}) async-start(bf16[8,512,512]{2,1,0:T(8,128)(2,1)} %bitcast.115), calls=%async_computation.1 | async-start | bytes 8388608 | tf_op jit(solution)/shard_map/all_to_all | solution.py:31
  248.5 83.0 %copy-start.4 = (bf16[2,512,512]{2,1,0:T(8,128)(2,1)S(1)}, bf16[2,512,512]{2,1,0:T(8,128)(2,1)}, u32[]{:S(2)}) copy-start(bf16[2,512,512]{2,1,0:T(8,128)(2,1)} %all-gather.7.cloned.1.call-done) | copy-start | bytes 3145732
  348.2 15.3 %copy-start.6 = (f32[64,256]{1,0:T(8,128)S(1)}, f32[64,256]{1,0:T(8,128)}, u32[]{:S(2)}) copy-start(f32[64,256]{1,0:T(8,128)} %param.25) | copy-start | bytes 196612
Sparse Core Ops, SparseCore 0:
  10.0 53.7 all-gather.6
  66.3 88.6 all-gather.8
  157.4 62.6 all-gather.10
  222.5 93.1 all-gather.12
